TPU v7x, 256 devices: a whole 4x4x8 slice. The times are simulated.
256 devices in a mesh: grid: 8 (over z), orb: 16 (over y, x_hi, core), pts: 2 (over x_lo).
Axes of the slice: x: 4 (x_hi: 2, x_lo: 2; x = x_hi * 2 + x_lo), y: 4, z: 8, core: 2. Of those that a mesh axis runs over, the one named last changes fastest.
Arguments:
- orbitals: bfloat16 [2048, 2048], P('grid', 'orb'), may hold values from -6 to 6
- points: int32 [8192], replicated, may hold values from 0 to 2047
- fitting: bfloat16 [2048, 8192], P('grid', ('orb', 'pts')), may hold values from -0.0625 to 0.0625
- screened: bfloat16 [8192, 8192], P(('orb', 'pts'), 'grid'), may hold values from -0.0014648438 to 0.0014648438
Outputs:
- exchange_orbitals: float32 [2048, 2048], P(('orb', 'pts'), 'grid')
- exchange_matrix: float32 [2048, 2048], P(('orb', 'pts'), 'grid')
Inputs may be any that keep to these rules, and one draw needn't show every extreme that they name: Grid rows of the window; two points may name the same row.
All inputs are finite; a program needn't handle non-finite values.
Results may differ from a plain program's by a relative error of at most 0.005.
Values may be sent and summed in bfloat16 or wider, within the bound.
No kernel may reach another device: no remote copies, remote signals or barrier semaphores. Data moves between devices by JAX's collectives and lax.ppermute only.
A program may use at most 128 MiB of HBM per device.

v0:
```python
import math
import jax
import jax.numpy as jnp
from jax import lax
from jax.sharding import Mesh, PartitionSpec as P

BF = jnp.bfloat16
F32 = jnp.float32
ORB = ("y", "xh", "core")
PLANE = ("y", "xh", "core", "pts")


def sent_to_all(x, axis):
    copies = jnp.broadcast_to(x, (lax.axis_size(axis), *x.shape))
    return lax.all_to_all(copies, axis, split_axis=0, concat_axis=0, tiled=True)


def per_device(orbitals, points, fitting, screened):
    n_grid = lax.axis_size("grid")
    n_plane = lax.axis_size(PLANE)
    grid_index = lax.axis_index("grid")
    plane_index = lax.axis_index(PLANE)
    rows_dev, width_dev = orbitals.shape
    nrows = rows_dev * n_grid
    nfull = width_dev * lax.axis_size(ORB)
    npoints = points.shape[0]
    row_block = npoints // n_plane
    column_block = npoints // n_grid
    share = nfull // (n_plane * n_grid)
    columns = sent_to_all(orbitals, "grid").reshape(nrows, width_dev)
    whole = lax.all_gather(columns, ORB, axis=1, tiled=True)
    fitted = sent_to_all(fitting, "grid").reshape(nrows, row_block)
    own = lax.dynamic_slice_in_dim(points, plane_index * row_block, row_block, 0)
    block = lax.dynamic_slice_in_dim(points, grid_index * column_block, column_block, 0)
    wanted = jnp.concatenate([own, block])
    rows = lax.broadcasted_iota(jnp.int32, (1, nrows), 1)
    choose = (wanted[:, None] == rows).astype(BF)
    picked = jnp.dot(choose, whole, preferred_element_type=F32).astype(BF)
    own_full, block_full = (picked[:row_block], picked[row_block:])
    density = lax.dot_general(
        own_full, block_full, (((1,), (1,)), ((), ())), preferred_element_type=F32
    )
    masked = (density * screened.astype(F32)).astype(BF)
    partial = lax.dot_general(
        block_full, masked, (((0,), (1,)), ((), ())), preferred_element_type=F32
    ).astype(BF)
    partial = partial.reshape(n_plane, n_grid, share, row_block).transpose(1, 0, 2, 3)
    parts = lax.all_to_all(partial, "grid", 0, 0, tiled=True)
    applied = jnp.sum(parts.astype(F32), axis=0).astype(BF)
    applied = applied.reshape(n_plane * share, row_block)
    terms = lax.dot_general(
        applied, fitted, (((1,), (1,)), ((), ())), preferred_element_type=F32
    ).astype(BF)
    parts = lax.all_to_all(terms.reshape(n_plane, share, nrows), PLANE, 0, 0, tiled=True)
    exchange = -jnp.sum(parts.astype(F32), axis=0)
    matrix = jnp.dot(exchange.astype(BF), whole, preferred_element_type=F32) / math.sqrt(nrows)
    both = jnp.stack(
        [exchange.reshape(share, n_grid, -1), matrix.reshape(share, n_grid, -1)]
    ).transpose(2, 0, 1, 3)
    both = lax.all_to_all(both, "grid", 0, 0, tiled=True)
    both = both.transpose(1, 0, 2, 3).reshape(2, n_grid * share, -1)
    return (both[0], both[1])


def solution(mesh):
    n_grid, n_orb, n_pts = (mesh.shape[a] for a in ("grid", "orb", "pts"))
    fine = Mesh(
        mesh.devices.reshape(n_grid, n_orb // 4, 2, 2, n_pts), ("grid", "y", "xh", "core", "pts")
    )
    in_specs = (P("grid", ORB), P(), P("grid", PLANE), P(PLANE, "grid"))
    out_specs = (P(PLANE, "grid"), P(PLANE, "grid"))
    return jax.shard_map(
        per_device, mesh=fine, in_specs=in_specs, out_specs=out_specs, check_vma=False
    )
```

profile of v0, /device:TPU:8, one launch (start us, length us, event | category | flops | bytes accessed | tf_op | source)
XLA Modules:
  0.0 246.3 jit_solution(5545429840203284281)
XLA Ops:
  7.2 0.0 all-gather.2.cloned.1.call-start
  7.2 0.9 broadcast_in_dim.7
  8.1 25.9 %all_to_all.25 = bf16[8,256,128]{2,1,0:T(8,128)(2,1)} all-to-all(bf16[8,256,128]{2,1,0:T(8,128)(2,1)S(1)} %broadcast_in_dim.7), channel_id=1, replica_groups=mesh['grid'=8,'y'=4,'xh'=2,'core'=2,'pts'=2] {'grid'}, dimensions={0} | all-to-all | bytes 1048576 | tf_op jit(solution)/shard_map/all_to_all | solution.py:15
  34.0 0.0 all-gather.2.cloned.1.call-update
  34.0 0.8 dynamic_slice.6
  34.8 0.7 dynamic_slice.7
  35.5 0.0 copy-start.1
  35.5 74.8 %all-gather.2.cloned.1.call-done = bf16[2048,2048]{1,0:T(8,128)(2,1)} async-done(((bf16[2048,128]{1,0:T(8,128)(2,1)}), bf16[2048,2048]{1,0:T(8,128)(2,1)}) %all-gather.2.cloned.1.call-update) | async-done | bytes 8388624 | tf_op jit(solution)/shard_map/all_gather | solution.py:31
  110.2 15.1 %fusion.1 = bf16[1280,2048]{1,0:T(8,128)(2,1)} fusion(bf16[2048,2048]{1,0:T(8,128)(2,1)} %all-gather.2.cloned.1.call-done, s32[1280]{0:T(1024)S(1)} %pad_add_fusion), kind=kOutput, calls=%fused_computation.2 | convolution fusion | flops 10742661120 | bytes 13636608 | tf_op jit(solution)/shard_map/dot_general | solution.py:38
  125.4 0.0 copy-done.1
  125.4 6.3 %fusion.7 = bf16[2048,256]{1,0:T(8,128)(2,1)S(1)} fusion(bf16[1280,2048]{1,0:T(8,128)(2,1)} %fusion.1, bf16[256,1024]{1,0:T(8,128)(2,1)S(1)} %copy-done.1), kind=kOutput, calls=%fused_computation.8 | convolution fusion | flops 2148794368 | bytes 11010048 | tf_op jit(solution)/shard_map/dot_general | solution.py:44
  131.7 0.1 copy.9
  131.7 36.0 %all_to_all.26 = bf16[8,32,8,256]{3,2,1,0:T(8,128)(2,1)S(1)} all-to-all(bf16[8,32,8,256]{3,2,1,0:T(8,128)(2,1)S(1)} %bitcast.26), channel_id=1, replica_groups=mesh['grid'=8,'y'=4,'xh'=2,'core'=2,'pts'=2] {'grid'}, dimensions={0} | all-to-all | bytes 2097152 | tf_op jit(solution)/shard_map/all_to_all | solution.py:48
  167.7 0.0 copy-done
  167.7 1.1 broadcast_in_dim.8
  168.8 3.6 %all-to-all-start.2 = ((bf16[8,256,256]{2,1,0:T(8,128)(2,1)}), bf16[8,256,256]{2,1,0:T(8,128)(2,1)S(1)}, u32[]{:S(2)}, u32[]{:S(2)}) async-start(bf16[8,256,256]{2,1,0:T(8,128)(2,1)} %broadcast_in_dim.8), calls=%async_computation.2 | async-start | bytes 2097152 | tf_op jit(solution)/shard_map/all_to_all | solution.py:15
  172.4 0.1 reduce_sum.21
  172.5 28.4 %all-to-all-done.2 = bf16[8,256,256]{2,1,0:T(8,128)(2,1)S(1)} async-done(((bf16[8,256,256]{2,1,0:T(8,128)(2,1)}), bf16[8,256,256]{2,1,0:T(8,128)(2,1)S(1)}, u32[]{:S(2)}, u32[]{:S(2)}) %all-to-all-start.2) | async-done | bytes 1048608 | tf_op jit(solution)/shard_map/all_to_all | solution.py:15
  200.9 0.5 fusion.10
  201.4 21.2 %all_to_all.27 = bf16[32,8,2048]{2,1,0:T(8,128)(2,1)S(1)} all-to-all(bf16[32,8,2048]{2,1,0:T(8,128)(2,1)S(1)} %fusion.10), channel_id=1, replica_groups=mesh['grid'=8,'y'=4,'xh'=2,'core'=2,'pts'=2] {'y','xh','core','pts'}, dimensions={0} | all-to-all | bytes 2097152 | tf_op jit(solution)/shard_map/all_to_all | solution.py:54
  222.6 0.2 convert_reduce_fusion
  222.8 4.6 %convolution_multiply_fusion = f32[8,2048]{1,0:T(8,128)S(1)} fusion(bf16[2048,2048]{1,0:T(8,128)(2,1)} %all-gather.2.cloned.1.call-done, f32[8,2048]{1,0:T(8,128)S(1)} %convert_reduce_fusion), kind=kOutput, calls=%fused_computation.11 | convolution fusion | flops 67158016 | bytes 8519680 | tf_op jit(solution)/shard_map/dot_general | solution.py:56
  227.4 11.5 %all_to_all.28 = f32[8,2,8,256]{3,2,1,0:T(8,128)S(1)} all-to-all(f32[8,2,8,256]{3,2,1,0:T(8,128)S(1)} %maximum_bitcast_fusion), channel_id=1, replica_groups=mesh['grid'=8,'y'=4,'xh'=2,'core'=2,'pts'=2] {'grid'}, dimensions={0} | all-to-all | bytes 262144 | tf_op jit(solution)/shard_map/all_to_all | solution.py:60
  238.8 0.7 slice_bitcast_fusion
  (4 shorter events, 0.0 us)
Async XLA Ops:
  7.2 103.1 %all-gather.2.cloned.1.call-start = ((), (), s32[]{:S(2)}) async-start(), calls=%async_computation.5 | async-start | bytes 8912896 | tf_op jit(solution)/shard_map/all_gather | solution.py:31
  35.5 89.9 %copy-start.1 = (bf16[256,1024]{1,0:T(8,128)(2,1)S(1)}, bf16[256,1024]{1,0:T(8,128)(2,1)}, u32[]{:S(2)}) copy-start(bf16[256,1024]{1,0:T(8,128)(2,1)} %param.7) | copy-start | bytes 1572868
  125.4 42.3 %copy-start = (bf16[256,256]{1,0:T(8,128)(2,1)S(1)}, bf16[256,256]{1,0:T(8,128)(2,1)}, u32[]{:S(2)}) copy-start(bf16[256,256]{1,0:T(8,128)(2,1)} %param.6) | copy-start | bytes 393220
  168.8 32.1 %all-to-all-start.2 = ((bf16[8,256,256]{2,1,0:T(8,128)(2,1)}), bf16[8,256,256]{2,1,0:T(8,128)(2,1)S(1)}, u32[]{:S(2)}, u32[]{:S(2)}) async-start(bf16[8,256,256]{2,1,0:T(8,128)(2,1)} %broadcast_in_dim.8), calls=%async_computation.2 | async-start | bytes 2097152 | tf_op jit(solution)/shard_map/all_to_all | solution.py:15
Sparse Core Ops, SparseCore 0:
  34.1 76.0 all-gather.1
where the time goes:
time: 247 us; the launch traced here: 246 us
  waiting for transfers between devices  103 us (42%)
  blocking collectives  94.5 us (38%)
  matrix products  26.5 us (11%)
  between operations  14.1 us (6%)
  local copies, waits for them, and re-layouts  4.22 us (2%)
  starting transfers between devices  3.59 us (1%)
    all_gather x1, waiting for transfers between devices, per_device(): whole = lax.all_gather(columns, ORB, axis=1, tiled=True)  74.8 us
    all_to_all x1, blocking collectives, per_device(): parts = lax.all_to_all(partial, 'grid', 0, 0, tiled=True)  36 us
    all_to_all x1, waiting for transfers between devices, sent_to_all(): return lax.all_to_all(copies, axis, split_axis=0, concat_axis=0, tiled=True)  28.4 us
    all_to_all x1, blocking collectives, sent_to_all(): return lax.all_to_all(copies, axis, split_axis=0, concat_axis=0, tiled=True)  25.9 us
    all_to_all x1, blocking collectives, per_device(): lax.all_to_all(terms.reshape(n_plane, share, nrows), PLANE, 0, 0, tiled=T...  21.2 us
    dot_general x1, matrix products, per_device(): picked = jnp.dot(choose, whole, preferred_element_type=F32).astype(BF)  15.1 us
    all_to_all x1, blocking collectives, per_device(): both = lax.all_to_all(both, 'grid', 0, 0, tiled=True)  11.5 us
    dot_general x1, matrix products, per_device(): lax.dot_general(block_full, masked, (((0,), (1,)), ((), ())), preferred_e...  6.29 us
  transfers between devices with their start and end apart: 2, of which 2 were waited for; matrix products, arithmetic and copies ran while one was open for 1% of the time, Pallas kernels for 0%

commit v1 on v0

--- a/solution.py
+++ b/solution.py
@@ -28,7 +28,9 @@
     column_block = npoints // n_grid
     share = nfull // (n_plane * n_grid)
     columns = sent_to_all(orbitals, "grid").reshape(nrows, width_dev)
-    whole = lax.all_gather(columns, ORB, axis=1, tiled=True)
+    whole = jnp.concatenate(
+        lax.all_to_all(jnp.stack([columns] * lax.axis_size(ORB)), ORB, 0, 0), axis=1
+    )
     fitted = sent_to_all(fitting, "grid").reshape(nrows, row_block)
     own = lax.dynamic_slice_in_dim(points, plane_index * row_block, row_block, 0)
     block = lax.dynamic_slice_in_dim(points, grid_index * column_block, column_block, 0)

time: 247 us -> 261 us (1.057)
  waiting for transfers between devices: 103 us -> 121 us
  between operations: 14.1 us -> 0.72 us
  starting transfers between devices: 3.59 us -> 10.9 us
  local copies, waits for them, and re-layouts: 4.22 us -> 9.07 us
  blocking collectives: 94.5 us -> 90.7 us
    all_to_all x0 -> x1, waiting for transfers between devices: none -> 93.8 us  [per_device(): lax.all_to_all(jnp.stack([columns] * lax.axis_size(ORB)), ORB, 0, 0)]
    all_gather x1 -> x0, waiting for transfers between devices: 74.8 us -> none  [per_device(): whole = lax.all_gather(columns, ORB, axis=1, tiled=True)]
    all_to_all x0 -> x1, starting transfers between devices: none -> 7.39 us  [per_device(): lax.all_to_all(jnp.stack([columns] * lax.axis_size(ORB)), ORB, 0, 0)]
    all_to_all x1, blocking collectives: 36 us -> 31.1 us  [per_device(): parts = lax.all_to_all(partial, 'grid', 0, 0, tiled=True)]
    another operation x0 -> x2, local copies, waits for them, and re-layouts: none -> 4.52 us  [per_device(): jnp.stack([columns] * lax.axis_size(ORB))]
where the time goes in v1:
time: 261 us; the launch traced here: 260 us
  waiting for transfers between devices  121 us (46%)
  blocking collectives  90.7 us (35%)
  matrix products  27.6 us (11%)
  starting transfers between devices  10.9 us (4%)
  local copies, waits for them, and re-layouts  9.07 us (3%)
    all_to_all x1, waiting for transfers between devices, per_device(): lax.all_to_all(jnp.stack([columns] * lax.axis_size(ORB)), ORB, 0, 0)  93.8 us
    all_to_all x1, blocking collectives, per_device(): parts = lax.all_to_all(partial, 'grid', 0, 0, tiled=True)  31.1 us
    all_to_all x1, waiting for transfers between devices, sent_to_all(): return lax.all_to_all(copies, axis, split_axis=0, concat_axis=0, tiled=True)  26.9 us
    all_to_all x1, blocking collectives, sent_to_all(): return lax.all_to_all(copies, axis, split_axis=0, concat_axis=0, tiled=True)  25.8 us
    all_to_all x1, blocking collectives, per_device(): lax.all_to_all(terms.reshape(n_plane, share, nrows), PLANE, 0, 0, tiled=T...  22.4 us
    dot_general x1, matrix products, per_device(): picked = jnp.dot(choose, whole, preferred_element_type=F32).astype(BF)  15.2 us
    all_to_all x1, blocking collectives, per_device(): both = lax.all_to_all(both, 'grid', 0, 0, tiled=True)  11.5 us
    all_to_all x1, starting transfers between devices, per_device(): lax.all_to_all(jnp.stack([columns] * lax.axis_size(ORB)), ORB, 0, 0)  7.39 us
  transfers between devices with their start and end apart: 2, of which 2 were waited for; matrix products, arithmetic and copies ran while one was open for 1% of the time, Pallas kernels for 0%

profile of v1, /device:TPU:8, one launch (start us, length us, event | category | flops | bytes accessed | tf_op | source)
XLA Modules:
  0.0 260.1 jit_solution(13964612611148998094)
XLA Ops:
  0.6 0.9 copy.10
  1.6 25.8 %all_to_all.30 = bf16[8,256,128]{1,2,0:T(8,128)(2,1)S(1)} all-to-all(bf16[8,256,128]{1,2,0:T(8,128)(2,1)S(1)} %broadcast_in_dim.7), channel_id=1, replica_groups=mesh['grid'=8,'y'=4,'xh'=2,'core'=2,'pts'=2] {'grid'}, dimensions={0} | all-to-all | bytes 1048576 | tf_op jit(solution)/shard_map/all_to_all | solution.py:15
  27.4 0.3 copy.11
  27.7 0.2 copy.12
  27.9 4.3 %stack.6 = bf16[16,2048,128]{1,2,0:T(8,128)(2,1)} broadcast(bf16[2048,128]{0,1:T(8,128)(2,1)S(1)} %copy.12), dimensions={1,2} | broadcast | bytes 8912896 | tf_op jit(solution)/shard_map/stack | solution.py:32
  32.2 7.4 %all-to-all-start.1 = ((bf16[16,2048,128]{1,2,0:T(8,128)(2,1)}), bf16[16,2048,128]{1,2,0:T(8,128)(2,1)}, u32[]{:S(2)}, u32[]{:S(2)}) async-start(bf16[16,2048,128]{1,2,0:T(8,128)(2,1)} %stack.6), calls=%async_computation.1 | async-start | bytes 16777216 | tf_op jit(solution)/shard_map/all_to_all | solution.py:32
  39.6 0.7 dynamic_slice.7
  40.3 0.8 dynamic_slice.6
  41.0 93.8 %all-to-all-done.1 = bf16[16,2048,128]{1,2,0:T(8,128)(2,1)} async-done(((bf16[16,2048,128]{1,2,0:T(8,128)(2,1)}), bf16[16,2048,128]{1,2,0:T(8,128)(2,1)}, u32[]{:S(2)}, u32[]{:S(2)}) %all-to-all-start.1) | async-done | bytes 8388640 | tf_op jit(solution)/shard_map/all_to_all | solution.py:32
  134.8 15.2 %fusion.1 = bf16[1280,2048]{1,0:T(8,128)(2,1)} fusion(bf16[2048,2048]{0,1:T(8,128)(2,1)} %bitcast.2, s32[1280]{0:T(1024)S(1)} %pad_add_fusion), kind=kOutput, calls=%fused_computation.2 | convolution fusion | flops 10742661120 | bytes 13636608 | tf_op jit(solution)/shard_map/dot_general | solution.py:40
  150.0 0.0 copy-done.1
  150.0 6.3 %fusion.7 = bf16[2048,256]{1,0:T(8,128)(2,1)S(1)} fusion(bf16[1280,2048]{1,0:T(8,128)(2,1)} %fusion.1, bf16[256,1024]{1,0:T(8,128)(2,1)S(1)} %copy-done.1), kind=kOutput, calls=%fused_computation.8 | convolution fusion | flops 2148794368 | bytes 11010048 | tf_op jit(solution)/shard_map/dot_general | solution.py:46
  156.3 0.1 copy.16
  156.4 31.1 %all_to_all.31 = bf16[8,32,8,256]{3,2,1,0:T(8,128)(2,1)S(1)} all-to-all(bf16[8,32,8,256]{3,2,1,0:T(8,128)(2,1)S(1)} %bitcast.29), channel_id=1, replica_groups=mesh['grid'=8,'y'=4,'xh'=2,'core'=2,'pts'=2] {'grid'}, dimensions={0} | all-to-all | bytes 2097152 | tf_op jit(solution)/shard_map/all_to_all | solution.py:50
  187.4 1.1 broadcast_in_dim.8
  188.6 3.6 %all-to-all-start.3 = ((bf16[8,256,256]{2,1,0:T(8,128)(2,1)}), bf16[8,256,256]{2,1,0:T(8,128)(2,1)S(1)}, u32[]{:S(2)}, u32[]{:S(2)}) async-start(bf16[8,256,256]{2,1,0:T(8,128)(2,1)} %broadcast_in_dim.8), calls=%async_computation.3 | async-start | bytes 2097152 | tf_op jit(solution)/shard_map/all_to_all | solution.py:15
  192.1 0.1 reduce_sum.21
  192.3 26.9 %all-to-all-done.3 = bf16[8,256,256]{2,1,0:T(8,128)(2,1)S(1)} async-done(((bf16[8,256,256]{2,1,0:T(8,128)(2,1)}), bf16[8,256,256]{2,1,0:T(8,128)(2,1)S(1)}, u32[]{:S(2)}, u32[]{:S(2)}) %all-to-all-start.3) | async-done | bytes 1048608 | tf_op jit(solution)/shard_map/all_to_all | solution.py:15
  219.2 0.5 fusion.10
  219.7 22.4 %all_to_all.32 = bf16[32,8,2048]{2,1,0:T(8,128)(2,1)S(1)} all-to-all(bf16[32,8,2048]{2,1,0:T(8,128)(2,1)S(1)} %fusion.10), channel_id=1, replica_groups=mesh['grid'=8,'y'=4,'xh'=2,'core'=2,'pts'=2] {'y','xh','core','pts'}, dimensions={0} | all-to-all | bytes 2097152 | tf_op jit(solution)/shard_map/all_to_all | solution.py:56
  242.1 0.2 convert_reduce_fusion
  242.3 5.6 %convolution_multiply_fusion = f32[8,2048]{1,0:T(8,128)S(1)} fusion(bf16[2048,2048]{0,1:T(8,128)(2,1)} %bitcast.2, f32[8,2048]{1,0:T(8,128)S(1)} %convert_reduce_fusion), kind=kOutput, calls=%fused_computation.11 | convolution fusion | flops 67158016 | bytes 8519680 | tf_op jit(solution)/shard_map/dot_general | solution.py:58
  248.0 11.5 %all_to_all.33 = f32[8,2,8,256]{3,2,1,0:T(8,128)S(1)} all-to-all(f32[8,2,8,256]{3,2,1,0:T(8,128)S(1)} %maximum_bitcast_fusion), channel_id=1, replica_groups=mesh['grid'=8,'y'=4,'xh'=2,'core'=2,'pts'=2] {'grid'}, dimensions={0} | all-to-all | bytes 262144 | tf_op jit(solution)/shard_map/all_to_all | solution.py:62
  259.4 0.7 slice_bitcast_fusion
  (7 shorter events, 0.1 us)
Async XLA Ops:
  32.2 102.6 %all-to-all-start.1 = ((bf16[16,2048,128]{1,2,0:T(8,128)(2,1)}), bf16[16,2048,128]{1,2,0:T(8,128)(2,1)}, u32[]{:S(2)}, u32[]{:S(2)}) async-start(bf16[16,2048,128]{1,2,0:T(8,128)(2,1)} %stack.6), calls=%async_computation.1 | async-start | bytes 16777216 | tf_op jit(solution)/shard_map/all_to_all | solution.py:32
  134.8 15.2 %copy-start.1 = (bf16[256,1024]{1,0:T(8,128)(2,1)S(1)}, bf16[256,1024]{1,0:T(8,128)(2,1)}, u32[]{:S(2)}) copy-start(bf16[256,1024]{1,0:T(8,128)(2,1)} %param.7) | copy-start | bytes 1572868
  150.0 37.5 %copy-start = (bf16[256,256]{1,0:T(8,128)(2,1)S(1)}, bf16[256,256]{1,0:T(8,128)(2,1)}, u32[]{:S(2)}) copy-start(bf16[256,256]{1,0:T(8,128)(2,1)} %param.6) | copy-start | bytes 393220
  188.6 30.7 %all-to-all-start.3 = ((bf16[8,256,256]{2,1,0:T(8,128)(2,1)}), bf16[8,256,256]{2,1,0:T(8,128)(2,1)S(1)}, u32[]{:S(2)}, u32[]{:S(2)}) async-start(bf16[8,256,256]{2,1,0:T(8,128)(2,1)} %broadcast_in_dim.8), calls=%async_computation.3 | async-start | bytes 2097152 | tf_op jit(solution)/shard_map/all_to_all | solution.py:15
